TPU v7x, 32 devices: a whole 2x2x4 slice. The times are simulated.
32 devices in a mesh: epoch: 8 (over z, y), blend: 4 (over x, core).
Axes of the slice: x: 2, y: 2, z: 4, core: 2. Of those that a mesh axis runs over, the one named last changes fastest.
Arguments:
- models: float32 [4, 16, 6, 4096], P('blend', 'epoch'), may hold values from -6 to 6
- observed: bfloat16 [8, 64, 4096], P('epoch', 'blend'), may hold values from -6 to 6
- weights: float32 [8, 64], P('epoch', 'blend'), may hold values from 0.5 to 2
- coverage: int32 [8, 64], P('epoch', 'blend'), may hold values from 0 to 1, as said below
- offsets: int32 [8, 64, 2], P('epoch', 'blend'), may hold values from 0 to 63
- counts: int32 [4, 16], P('blend', 'epoch'), may hold values from 1 to 8, as said below
- psf_y: bfloat16 [8, 4096], P('epoch'), may hold values from -0.75 to 0.75
- resample_y: bfloat16 [8, 4096], P('epoch'), may hold values from -0.75 to 0.75
- psf_x: bfloat16 [8, 4096], P('epoch'), may hold values from -0.75 to 0.75
- resample_x: bfloat16 [8, 4096], P('epoch'), may hold values from -0.75 to 0.75
Outputs:
- updated: float32 [4, 16, 6, 4096], P('blend', 'epoch')
Inputs may be any that keep to these rules, and one draw needn't show every extreme that they name: `coverage`: every blend is seen by one epoch or more. counts of blend b is the sum of coverage over all epochs for b.
All inputs are finite; a program needn't handle non-finite values.
Results may differ from a plain program's by a relative error of at most 0.0017.
Values may be sent and summed in bfloat16 or wider, within the bound.
A program may use at most 128 MiB of HBM per device.

v0:
```python
import jax
import jax.numpy as jnp
from jax import lax
from jax.sharding import PartitionSpec as P

CUT = 64
BANDS = 6
PIX2 = 4096
step_size = 0.5


def roll_forward(image, down, across):
    side = image.shape[0]
    doubled = jnp.concatenate([image, image], axis=0)
    rows = lax.dynamic_slice_in_dim(doubled, down, side, 0)
    doubled = jnp.concatenate([rows, rows], axis=1)
    return lax.dynamic_slice_in_dim(doubled, across, side, 1)


def one_epoch(model_low, observed, scale, offsets, left, right, band):
    side = left.shape[0]
    count = observed.shape[0]
    chosen = lax.dynamic_index_in_dim(model_low, band, 1, keepdims=False)
    shifted = jax.vmap(roll_forward)(chosen, offsets[:, 0], offsets[:, 1])
    blurred = jnp.einsum("ij,bjk->bik", left, shifted, preferred_element_type=jnp.float32).astype(
        jnp.bfloat16
    )
    predicted = jnp.einsum("bik,lk->bil", blurred, right, preferred_element_type=jnp.float32)
    target = observed.reshape(count, side, side).astype(jnp.float32)
    misfit = (scale[:, None, None] * (predicted - target)).astype(jnp.bfloat16)
    back = jnp.einsum("ji,bjk->bik", left, misfit, preferred_element_type=jnp.float32).astype(
        jnp.bfloat16
    )
    term = jnp.einsum("bik,kl->bil", back, right, preferred_element_type=jnp.float32)
    return jax.vmap(roll_forward)(term, side - offsets[:, 0], side - offsets[:, 1])


def on_device(
    models, observed, weights, coverage, offsets, counts, psf_y, resample_y, psf_x, resample_x
):
    ep_dev = observed.shape[0]
    group_size = lax.axis_size("epoch")
    all_epochs = ep_dev * group_size
    anchor = lax.axis_index("epoch") * ep_dev
    lefts = jnp.einsum(
        "eij,ejk->eik",
        psf_y.reshape(ep_dev, CUT, CUT),
        resample_y.reshape(ep_dev, CUT, CUT),
        preferred_element_type=jnp.float32,
    ).astype(jnp.bfloat16)
    rights = jnp.einsum(
        "eij,ejk->eik",
        psf_x.reshape(ep_dev, CUT, CUT),
        resample_x.reshape(ep_dev, CUT, CUT),
        preferred_element_type=jnp.float32,
    ).astype(jnp.bfloat16)
    scale = weights * coverage.astype(jnp.float32)
    epoch_bands = (anchor + 0) * BANDS // all_epochs
    first_band = anchor * BANDS // all_epochs
    model_low = models.astype(jnp.bfloat16)
    piece = lax.all_gather(model_low, "epoch", axis=1, tiled=True)
    count = piece.shape[1]
    blocks = piece[0].reshape(count, BANDS, CUT, CUT)
    terms = one_epoch(
        blocks, observed[0], scale[0], offsets[0], lefts[0], rights[0], epoch_bands
    ).reshape(count, PIX2)
    total = jnp.zeros((count, 2, PIX2), jnp.float32)
    slot = epoch_bands - first_band
    current = lax.dynamic_index_in_dim(total, slot, 1, keepdims=False)
    total = lax.dynamic_update_index_in_dim(total, current + terms, slot, 1)
    received = lax.all_to_all(total, "epoch", split_axis=0, concat_axis=1, tiled=True)
    slot_count = received.shape[1]
    position = jnp.arange(slot_count, dtype=jnp.int32)
    source = position // 2
    band_of = source * ep_dev * BANDS // all_epochs + position % 2
    selector = (band_of[:, None] == jnp.arange(BANDS, dtype=jnp.int32)[None, :]).astype(jnp.float32)
    gradient = jnp.einsum("bkp,kc->bcp", received, selector, precision=lax.Precision.HIGHEST)
    divisor = counts[0].astype(jnp.float32)[:, None, None]
    updated = models[0] - step_size * gradient / divisor
    return updated[None]


def solution(mesh):
    return jax.shard_map(
        on_device,
        mesh=mesh,
        in_specs=(
            P("blend", "epoch", None, None),
            P("epoch", "blend", None),
            P("epoch", "blend"),
            P("epoch", "blend"),
            P("epoch", "blend", None),
            P("blend", "epoch"),
            P("epoch", None),
            P("epoch", None),
            P("epoch", None),
            P("epoch", None),
        ),
        out_specs=P("blend", "epoch", None, None),
        check_vma=False,
    )
```

profile of v0, /device:TPU:0, one launch (start us, length us, event | category | flops | bytes accessed | tf_op | source)
XLA Modules:
  0.0 66.9 jit_solution(17146201242047359278)
XLA Ops:
  0.0 1.0 %convert_element_type.47 = bf16[1,2,6,4096]{3,1,2,0:T(2,128)(2,1)S(1)} convert(f32[1,2,6,4096]{3,1,2,0:T(2,128)} %param.10) | non-fusion elementwise | flops 49152 | bytes 294912 | tf_op jit(solution)/shard_map/convert_element_type | solution.py:60
  1.0 0.1 copy.60
  1.1 34.6 %all_gather.3 = bf16[1,16,6,4096]{3,2,0,1:T(8,128)(2,1)S(1)} all-gather(bf16[1,2,6,4096]{3,2,0,1:T(8,128)(2,1)S(1)} %copy.60), channel_id=1, replica_groups=mesh['epoch'=8,'blend'=4] {'epoch'}, dimensions={1}, use_global_device_ids=true | all-gather | bytes 884736 | tf_op jit(solution)/shard_map/all_gather | solution.py:61
  35.7 0.4 copy.61
  36.1 0.0 copy-start.6
  36.1 1.7 %reshape_squeeze.4 = bf16[16,6,64,64]{3,2,0,1:T(8,128)(2,1)S(1)} reshape(bf16[1,16,6,4096]{3,1,2,0:T(8,128)(2,1)S(1)} %copy.61) | data formatting | bytes 1572864 | tf_op jit(solution)/shard_map/reshape;squeeze | solution.py:63
  37.9 0.2 copy.86
  38.1 0.1 pad_maximum_fusion
  38.2 0.0 copy-done.6
  38.2 0.0 copy-start.2
  38.2 0.0 copy-start.3
  38.2 0.0 copy-start.4
  38.2 0.0 copy-start.5
  38.3 0.0 copy-start.1
  38.3 1.4 %gather_fusion = bf16[16,64,64]{2,0,1:T(8,128)(2,1)S(1)} fusion(bf16[16,128,64]{2,0,1:T(8,128)(2,1)S(1)} %pad_maximum_fusion, s32[16]{0:T(128)S(1)} %get-tuple-element.6), kind=kCustom, calls=%fused_computation | custom fusion | bytes 262336 | tf_op jit(solution)/shard_map/vmap()/gather | solution.py:15
  39.6 0.1 pad_maximum_fusion.3
  39.8 0.5 copy.63
  40.4 0.1 reduce.2
  40.4 0.1 reshape.76
  40.5 0.1 reduce.3
  40.5 0.1 reshape.77
  40.6 0.1 reduce
  40.7 0.1 reshape.74
  40.8 0.1 reduce.1
  40.8 0.0 copy-start.7
  40.8 0.0 copy-start.8
  40.9 0.1 reshape.75
  40.9 0.2 reshape.78
  41.2 1.4 %gather_fusion.1 = bf16[16,64,64]{1,0,2:T(8,128)(2,1)S(1)} fusion(bf16[16,64,128]{1,0,2:T(8,128)(2,1)S(1)} %copy.63, s32[16]{0:T(128)S(1)} %get-tuple-element.7), kind=kCustom, calls=%fused_computation.1 | custom fusion | bytes 262336 | tf_op jit(solution)/shard_map/vmap()/gather | solution.py:17
  42.5 0.1 fusion.10
  42.7 0.1 fusion.9
  42.8 0.4 fusion.5
  43.3 0.4 fusion.8
  43.7 0.2 pad_maximum_fusion.1
  43.9 0.5 copy.69
  44.4 1.3 %gather_fusion.2 = f32[16,64,64]{2,0,1:T(8,128)S(1)} fusion(f32[16,128,64]{2,0,1:T(8,128)S(1)} %copy.69, s32[16]{0:T(128)S(1)} %get-tuple-element.8), kind=kCustom, calls=%fused_computation.2 | custom fusion | bytes 524480 | tf_op jit(solution)/shard_map/vmap()/gather | solution.py:15
  45.8 0.2 pad_maximum_fusion.2
  46.0 0.6 copy.70
  46.6 1.3 %gather_fusion.3 = f32[16,64,64]{1,0,2:T(8,128)S(1)} fusion(f32[16,64,128]{1,0,2:T(8,128)S(1)} %copy.70, s32[16]{0:T(128)S(1)} %get-tuple-element.5), kind=kCustom, calls=%fused_computation.3 | custom fusion | bytes 524480 | tf_op jit(solution)/shard_map/vmap()/gather | solution.py:17
  47.9 0.3 copy.71
  48.2 0.0 copy-start.9
  48.2 0.3 broadcast_in_dim.8
  48.5 1.0 %dynamic_update_slice.4.clone = f32[16,2,4096]{2,1,0:T(2,128)} pad(f32[16,1,4096]{2,1,0:T(1,128)S(1)} %broadcast_in_dim.8, f32[]{:T(128)} %constant.85.clone.1), padding=0_0x0_1x0_0 | pad | bytes 786436 | tf_op jit(solution)/shard_map/jit(dynamic_update_index_in_dim)/dynamic_update_slice | solution.py:70
  49.5 5.5 %all-to-all-start = ((f32[16,2,4096]{2,1,0:T(2,128)}), f32[16,2,4096]{2,1,0:T(2,128)S(1)}, u32[]{:S(2)}, u32[]{:S(2)}) async-start(f32[16,2,4096]{2,1,0:T(2,128)} %dynamic_update_slice.4.clone), calls=%async_computation | async-start | bytes 1048576 | tf_op jit(solution)/shard_map/all_to_all | solution.py:71
  55.0 10.3 %all-to-all-done = f32[16,2,4096]{2,1,0:T(2,128)S(1)} async-done(((f32[16,2,4096]{2,1,0:T(2,128)}), f32[16,2,4096]{2,1,0:T(2,128)S(1)}, u32[]{:S(2)}, u32[]{:S(2)}) %all-to-all-start) | async-done | bytes 524320 | tf_op jit(solution)/shard_map/all_to_all | solution.py:71
  65.3 0.4 all_to_all.16
  65.7 0.4 fusion.3
  66.1 0.8 %copy.74 = f32[1,2,6,4096]{3,1,2,0:T(2,128)} copy(f32[1,2,6,4096]{3,2,1,0:T(8,128)S(1)} %fusion.3) | data formatting | bytes 393216 | tf_op jit(solution)/shard_map/broadcast_in_dim | solution.py:80
  (16 shorter events, 0.1 us)
Async XLA Ops:
  36.1 2.1 %copy-start.6 = (s32[1,16,2]{1,2,0:T(2,128)S(1)}, s32[1,16,2]{1,2,0:T(2,128)}, u32[]{:S(2)}) copy-start(s32[1,16,2]{1,2,0:T(2,128)} %param.14) | copy-start | bytes 388
  38.2 2.1 %copy-start.2 = (bf16[1,4096]{1,0:T(2,128)(2,1)S(1)}, bf16[1,4096]{1,0:T(2,128)(2,1)}, u32[]{:S(2)}) copy-start(bf16[1,4096]{1,0:T(2,128)(2,1)} %param.18) | copy-start | bytes 24580
  38.2 2.3 %copy-start.3 = (bf16[1,4096]{1,0:T(2,128)(2,1)S(1)}, bf16[1,4096]{1,0:T(2,128)(2,1)}, u32[]{:S(2)}) copy-start(bf16[1,4096]{1,0:T(2,128)(2,1)} %param.19) | copy-start | bytes 24580
  38.2 2.4 %copy-start.4 = (bf16[1,4096]{1,0:T(2,128)(2,1)S(1)}, bf16[1,4096]{1,0:T(2,128)(2,1)}, u32[]{:S(2)}) copy-start(bf16[1,4096]{1,0:T(2,128)(2,1)} %param.16) | copy-start | bytes 24580
  38.2 2.5 %copy-start.5 = (bf16[1,4096]{1,0:T(2,128)(2,1)S(1)}, bf16[1,4096]{1,0:T(2,128)(2,1)}, u32[]{:S(2)}) copy-start(bf16[1,4096]{1,0:T(2,128)(2,1)} %param.17) | copy-start | bytes 24580
  38.3 2.7 %copy-start.1 = (bf16[1,16,4096]{2,1,0:T(8,128)(2,1)S(1)}, bf16[1,16,4096]{2,1,0:T(8,128)(2,1)}, u32[]{:S(2)}) copy-start(bf16[1,16,4096]{2,1,0:T(8,128)(2,1)} %param.11) | copy-start | bytes 393220
  40.8 2.0 %copy-start.7 = (f32[1,16]{1,0:T(1,128)S(1)}, f32[1,16]{1,0:T(1,128)}, u32[]{:S(2)}) copy-start(f32[1,16]{1,0:T(1,128)} %param.12) | copy-start | bytes 196
  40.8 1.9 %copy-start.8 = (s32[1,16]{1,0:T(1,128)S(1)}, s32[1,16]{1,0:T(1,128)}, u32[]{:S(2)}) copy-start(s32[1,16]{1,0:T(1,128)} %param.13) | copy-start | bytes 196
  48.2 6.9 %copy-start.9 = (s32[1,2]{1,0:T(1,128)S(1)}, s32[1,2]{1,0:T(1,128)}, u32[]{:S(2)}) copy-start(s32[1,2]{1,0:T(1,128)} %param.15) | copy-start | bytes 28
  49.5 16.2 %copy-start = (f32[1,2,6,4096]{3,1,2,0:T(2,128)S(1)}, f32[1,2,6,4096]{3,1,2,0:T(2,128)}, u32[]{:S(2)}) copy-start(f32[1,2,6,4096]{3,1,2,0:T(2,128)} %param.10) | copy-start | bytes 589828
  49.5 15.8 %all-to-all-start = ((f32[16,2,4096]{2,1,0:T(2,128)}), f32[16,2,4096]{2,1,0:T(2,128)S(1)}, u32[]{:S(2)}, u32[]{:S(2)}) async-start(f32[16,2,4096]{2,1,0:T(2,128)} %dynamic_update_slice.4.clone), calls=%async_computation | async-start | bytes 1048576 | tf_op jit(solution)/shard_map/all_to_all | solution.py:71
where the time goes:
time: 67.1 us; the launch traced here: 66.9 us
  blocking collectives  34.6 us (52%)
  local copies, waits for them, and re-layouts  12.8 us (19%)
  waiting for transfers between devices  10.3 us (15%)
  starting transfers between devices  5.52 us (8%)
  other arithmetic  1.9 us (3%)
  matrix products  1.48 us (2%)
    all_gather x1, blocking collectives, on_device(): piece = lax.all_gather(model_low, 'epoch', axis=1, tiled=True)  34.6 us
    all_to_all x1, waiting for transfers between devices, on_device(): lax.all_to_all(total, 'epoch', split_axis=0, concat_axis=1, tiled=True)  10.3 us
    all_to_all x1, starting transfers between devices, on_device(): lax.all_to_all(total, 'epoch', split_axis=0, concat_axis=1, tiled=True)  5.52 us
    gather x3, local copies, waits for them, and re-layouts, roll_forward(): return lax.dynamic_slice_in_dim(doubled, across, side, 1)  2.97 us
    gather x2, local copies, waits for them, and re-layouts, roll_forward(): rows = lax.dynamic_slice_in_dim(doubled, down, side, 0)  2.71 us
    another operation x1, local copies, waits for them, and re-layouts, on_device(): blocks = piece[0].reshape(count, BANDS, CUT, CUT)  1.72 us
  transfers between devices with their start and end apart: 1, of which 1 were waited for; matrix products, arithmetic and copies ran while one was open for 0% of the time, Pallas kernels for 0%

commit v1 on v0

--- a/solution.py
+++ b/solution.py
@@ -58,7 +58,9 @@
     epoch_bands = (anchor + 0) * BANDS // all_epochs
     first_band = anchor * BANDS // all_epochs
     model_low = models.astype(jnp.bfloat16)
-    piece = lax.all_gather(model_low, "epoch", axis=1, tiled=True)
+    piece = jnp.concatenate(
+        lax.all_to_all(jnp.stack([model_low] * lax.axis_size("epoch")), "epoch", 0, 0), axis=1
+    )
     count = piece.shape[1]
     blocks = piece[0].reshape(count, BANDS, CUT, CUT)
     terms = one_epoch(

time: 67.1 us -> 62.9 us (0.937)
  blocking collectives: 34.6 us -> 0 us
  waiting for transfers between devices: 10.3 us -> 32.9 us
  starting transfers between devices: 5.52 us -> 11 us
  local copies, waits for them, and re-layouts: 12.8 us -> 14.9 us
    all_gather x1 -> x0, blocking collectives: 34.6 us -> none  [on_device(): piece = lax.all_gather(model_low, 'epoch', axis=1, tiled=True)]
    all_to_all x0 -> x1, waiting for transfers between devices: none -> 18.3 us  [on_device(): lax.all_to_all(jnp.stack([model_low] * lax.axis_size('epoch')), 'epoch',...]
    all_to_all x0 -> x1, starting transfers between devices: none -> 7.33 us  [on_device(): lax.all_to_all(jnp.stack([model_low] * lax.axis_size('epoch')), 'epoch',...]
    all_to_all x1, waiting for transfers between devices: 10.3 us -> 14.6 us  [on_device(): lax.all_to_all(total, 'epoch', split_axis=0, concat_axis=1, tiled=True)]
    all_to_all x1, starting transfers between devices: 5.52 us -> 3.7 us  [on_device(): lax.all_to_all(total, 'epoch', split_axis=0, concat_axis=1, tiled=True)]
    another operation x3 -> x5, local copies, waits for them, and re-layouts: 0.25 us -> 1.98 us  [the longest x1 1.65 us: on_device(): jnp.stack([model_low] * lax.axis_size('epoch'))]
    convert_element_type x1, local copies, waits for them, and re-layouts: 0.21 us -> 1.02 us  [one_epoch(): target = observed.reshape(count, side, side).astype(jnp.float32)]
    all_to_all x0 -> x1, local copies, waits for them, and re-layouts: none -> 0.78 us  [on_device(): lax.all_to_all(jnp.stack([model_low] * lax.axis_size('epoch')), 'epoch',...]
  transfers between devices with their start and end apart: 1 -> 2, of which waited for: 1 -> 2; matrix products, arithmetic and copies ran while one was open for 0% -> 3% of each run, Pallas kernels for 0% -> 0%
where the time goes in v1:
time: 62.9 us; the launch traced here: 62.6 us
  waiting for transfers between devices  32.9 us (52%)
  local copies, waits for them, and re-layouts  14.9 us (24%)
  starting transfers between devices  11 us (17%)
  other arithmetic  1.96 us (3%)
  matrix products  1.48 us (2%)
    all_to_all x1, waiting for transfers between devices, on_device(): lax.all_to_all(jnp.stack([model_low] * lax.axis_size('epoch')), 'epoch',...  18.3 us
    all_to_all x1, waiting for transfers between devices, on_device(): lax.all_to_all(total, 'epoch', split_axis=0, concat_axis=1, tiled=True)  14.6 us
    all_to_all x1, starting transfers between devices, on_device(): lax.all_to_all(jnp.stack([model_low] * lax.axis_size('epoch')), 'epoch',...  7.33 us
    all_to_all x1, starting transfers between devices, on_device(): lax.all_to_all(total, 'epoch', split_axis=0, concat_axis=1, tiled=True)  3.7 us
    gather x3, local copies, waits for them, and re-layouts, roll_forward(): return lax.dynamic_slice_in_dim(doubled, across, side, 1)  2.97 us
    gather x2, local copies, waits for them, and re-layouts, roll_forward(): rows = lax.dynamic_slice_in_dim(doubled, down, side, 0)  2.71 us
    another operation x1, local copies, waits for them, and re-layouts, on_device(): jnp.stack([model_low] * lax.axis_size('epoch'))  1.65 us
  transfers between devices with their start and end apart: 2, of which 2 were waited for; matrix products, arithmetic and copies ran while one was open for 3% of the time, Pallas kernels for 0%

profile of v1, /device:TPU:0, one launch (start us, length us, event | category | flops | bytes accessed | tf_op | source)
XLA Modules:
  0.0 62.6 jit_solution(17851898040963915639)
XLA Ops:
  0.0 1.1 %convert_bitcast_fusion = bf16[2,6,4096]{2,0,1:T(2,128)(2,1)S(1)} fusion(f32[1,2,6,4096]{3,1,2,0:T(2,128)} %param.10), kind=kLoop, calls=%fused_computation.27 | loop fusion | flops 49152 | bytes 294912 | tf_op jit(solution)/shard_map/convert_element_type | solution.py:60
  1.1 0.0 copy-start.8
  1.1 0.0 copy-start.9
  1.1 0.0 copy-start.7
  1.1 1.7 %stack.2 = bf16[8,1,2,6,4096]{4,2,3,1,0:T(2,128)(2,1)} broadcast(bf16[2,6,4096]{2,0,1:T(2,128)(2,1)S(1)} %convert_bitcast_fusion), dimensions={2,3,4} | broadcast | bytes 884736 | tf_op jit(solution)/shard_map/stack | solution.py:62
  2.8 7.3 %all-to-all-start = ((bf16[8,1,2,6,4096]{4,2,3,1,0:T(2,128)(2,1)}), bf16[8,1,2,6,4096]{4,2,3,1,0:T(2,128)(2,1)S(1)}, u32[]{:S(2)}, u32[]{:S(2)}) async-start(bf16[8,1,2,6,4096]{4,2,3,1,0:T(2,128)(2,1)} %stack.2), calls=%async_computation | async-start | bytes 1572864 | tf_op jit(solution)/shard_map/all_to_all | solution.py:62
  10.1 0.0 copy-done.3
  10.1 0.1 reduce.2
  10.1 0.1 reshape.79
  10.2 0.0 copy-done.4
  10.2 0.1 reduce.3
  10.3 0.1 reshape.80
  10.4 0.0 copy-done.5
  10.4 0.1 reduce
  10.4 0.1 reshape.77
  10.5 0.0 copy-done.6
  10.5 0.1 reduce.1
  10.6 0.1 reshape.78
  10.7 1.0 %reshape.81 = f32[16,64,64]{2,1,0:T(8,128)} reshape(bf16[1,16,4096]{2,1,0:T(8,128)(2,1)S(1)} %copy-done.2) | data formatting | bytes 393216 | tf_op jit(solution)/shard_map/convert_element_type | solution.py:29
  11.7 0.1 fusion.10
  11.8 0.1 fusion.9
  12.0 18.3 %all-to-all-done = bf16[8,1,2,6,4096]{4,2,3,1,0:T(2,128)(2,1)S(1)} async-done(((bf16[8,1,2,6,4096]{4,2,3,1,0:T(2,128)(2,1)}), bf16[8,1,2,6,4096]{4,2,3,1,0:T(2,128)(2,1)S(1)}, u32[]{:S(2)}, u32[]{:S(2)}) %all-to-all-start) | async-done | bytes 786464 | tf_op jit(solution)/shard_map/all_to_all | solution.py:62
  30.3 0.8 %copy.29 = bf16[8,1,2,6,4096]{4,2,0,3,1:T(2,128)(2,1)S(1)} copy(bf16[8,1,2,6,4096]{4,2,3,1,0:T(2,128)(2,1)S(1)} %all-to-all-done) | data formatting | bytes 1572864 | tf_op jit(solution)/shard_map/all_to_all | solution.py:62
  31.0 1.0 %reshape_squeeze_reshape.3 = bf16[16,6,64,64]{3,2,0,1:T(8,128)(2,1)S(1)} reshape(bf16[8,1,2,6,4096]{4,2,0,3,1:T(2,128)(2,1)S(1)} %copy.29) | data formatting | bytes 1572864 | tf_op jit(solution)/shard_map/reshape;squeeze;reshape | solution.py:65
  32.1 0.2 copy.54
  32.3 0.1 pad_maximum_fusion
  32.4 1.4 %gather_fusion = bf16[16,64,64]{2,0,1:T(8,128)(2,1)S(1)} fusion(bf16[16,128,64]{2,0,1:T(8,128)(2,1)S(1)} %pad_maximum_fusion, s32[16]{0:T(128)S(1)} %get-tuple-element.6), kind=kCustom, calls=%fused_computation | custom fusion | bytes 262336 | tf_op jit(solution)/shard_map/vmap()/gather | solution.py:15
  33.8 0.1 pad_maximum_fusion.3
  33.9 0.0 copy-start
  34.0 0.5 copy.31
  34.5 1.4 %gather_fusion.1 = bf16[16,64,64]{1,0,2:T(8,128)(2,1)S(1)} fusion(bf16[16,64,128]{1,0,2:T(8,128)(2,1)S(1)} %copy.31, s32[16]{0:T(128)S(1)} %get-tuple-element.7), kind=kCustom, calls=%fused_computation.1 | custom fusion | bytes 262336 | tf_op jit(solution)/shard_map/vmap()/gather | solution.py:17
  35.9 0.4 fusion.5
  36.3 0.4 fusion.8
  36.8 0.2 pad_maximum_fusion.1
  37.0 0.5 copy.37
  37.5 1.3 %gather_fusion.2 = f32[16,64,64]{2,0,1:T(8,128)S(1)} fusion(f32[16,128,64]{2,0,1:T(8,128)S(1)} %copy.37, s32[16]{0:T(128)S(1)} %get-tuple-element.8), kind=kCustom, calls=%fused_computation.2 | custom fusion | bytes 524480 | tf_op jit(solution)/shard_map/vmap()/gather | solution.py:15
  38.8 0.2 pad_maximum_fusion.2
  39.0 0.6 copy.38
  39.6 1.3 %gather_fusion.3 = f32[16,64,64]{1,0,2:T(8,128)S(1)} fusion(f32[16,64,128]{1,0,2:T(8,128)S(1)} %copy.38, s32[16]{0:T(128)S(1)} %get-tuple-element.5), kind=kCustom, calls=%fused_computation.3 | custom fusion | bytes 524480 | tf_op jit(solution)/shard_map/vmap()/gather | solution.py:17
  41.0 0.3 copy.39
  41.2 0.0 copy-start.10
  41.3 0.3 broadcast_in_dim.8
  41.6 1.0 %dynamic_update_slice.4.clone = f32[16,2,4096]{2,1,0:T(2,128)} pad(f32[16,1,4096]{2,1,0:T(1,128)S(1)} %broadcast_in_dim.8, f32[]{:T(128)} %constant.85.clone.1), padding=0_0x0_1x0_0 | pad | bytes 786436 | tf_op jit(solution)/shard_map/jit(dynamic_update_index_in_dim)/dynamic_update_slice | solution.py:72
  42.6 3.7 %all-to-all-start.1 = ((f32[16,2,4096]{2,1,0:T(2,128)}), f32[16,2,4096]{2,1,0:T(2,128)S(1)}, u32[]{:S(2)}, u32[]{:S(2)}) async-start(f32[16,2,4096]{2,1,0:T(2,128)} %dynamic_update_slice.4.clone), calls=%async_computation.1 | async-start | bytes 1048576 | tf_op jit(solution)/shard_map/all_to_all | solution.py:73
  46.3 14.6 %all-to-all-done.1 = f32[16,2,4096]{2,1,0:T(2,128)S(1)} async-done(((f32[16,2,4096]{2,1,0:T(2,128)}), f32[16,2,4096]{2,1,0:T(2,128)S(1)}, u32[]{:S(2)}, u32[]{:S(2)}) %all-to-all-start.1) | async-done | bytes 524320 | tf_op jit(solution)/shard_map/all_to_all | solution.py:73
  61.0 0.4 all_to_all.20
  61.4 0.4 fusion.3
  61.7 0.8 %copy.42 = f32[1,2,6,4096]{3,1,2,0:T(2,128)} copy(f32[1,2,6,4096]{3,2,1,0:T(8,128)S(1)} %fusion.3) | data formatting | bytes 393216 | tf_op jit(solution)/shard_map/broadcast_in_dim | solution.py:82
  (19 shorter events, 0.1 us)
Async XLA Ops:
  0.0 10.1 %copy-start.3 = (bf16[1,4096]{1,0:T(2,128)(2,1)S(1)}, bf16[1,4096]{1,0:T(2,128)(2,1)}, u32[]{:S(2)}) copy-start(bf16[1,4096]{1,0:T(2,128)(2,1)} %param.18) | copy-start | bytes 24580
  0.0 10.2 %copy-start.4 = (bf16[1,4096]{1,0:T(2,128)(2,1)S(1)}, bf16[1,4096]{1,0:T(2,128)(2,1)}, u32[]{:S(2)}) copy-start(bf16[1,4096]{1,0:T(2,128)(2,1)} %param.19) | copy-start | bytes 24580
  0.0 10.4 %copy-start.5 = (bf16[1,4096]{1,0:T(2,128)(2,1)S(1)}, bf16[1,4096]{1,0:T(2,128)(2,1)}, u32[]{:S(2)}) copy-start(bf16[1,4096]{1,0:T(2,128)(2,1)} %param.16) | copy-start | bytes 24580
  0.0 10.5 %copy-start.6 = (bf16[1,4096]{1,0:T(2,128)(2,1)S(1)}, bf16[1,4096]{1,0:T(2,128)(2,1)}, u32[]{:S(2)}) copy-start(bf16[1,4096]{1,0:T(2,128)(2,1)} %param.17) | copy-start | bytes 24580
  0.0 10.6 %copy-start.2 = (bf16[1,16,4096]{2,1,0:T(8,128)(2,1)S(1)}, bf16[1,16,4096]{2,1,0:T(8,128)(2,1)}, u32[]{:S(2)}) copy-start(bf16[1,16,4096]{2,1,0:T(8,128)(2,1)} %param.11) | copy-start | bytes 393220
  1.1 10.8 %copy-start.8 = (f32[1,16]{1,0:T(1,128)S(1)}, f32[1,16]{1,0:T(1,128)}, u32[]{:S(2)}) copy-start(f32[1,16]{1,0:T(1,128)} %param.12) | copy-start | bytes 196
  1.1 10.8 %copy-start.9 = (s32[1,16]{1,0:T(1,128)S(1)}, s32[1,16]{1,0:T(1,128)}, u32[]{:S(2)}) copy-start(s32[1,16]{1,0:T(1,128)} %param.13) | copy-start | bytes 196
  1.1 10.8 %copy-start.7 = (s32[1,16,2]{1,2,0:T(2,128)S(1)}, s32[1,16,2]{1,2,0:T(2,128)}, u32[]{:S(2)}) copy-start(s32[1,16,2]{1,2,0:T(2,128)} %param.14) | copy-start | bytes 388
  2.8 27.5 %all-to-all-start = ((bf16[8,1,2,6,4096]{4,2,3,1,0:T(2,128)(2,1)}), bf16[8,1,2,6,4096]{4,2,3,1,0:T(2,128)(2,1)S(1)}, u32[]{:S(2)}, u32[]{:S(2)}) async-start(bf16[8,1,2,6,4096]{4,2,3,1,0:T(2,128)(2,1)} %stack.2), calls=%async_computation | async-start | bytes 1572864 | tf_op jit(solution)/shard_map/all_to_all | solution.py:62
  33.9 1.9 %copy-start = (f32[16,64,64]{2,1,0:T(8,128)S(1)}, f32[16,64,64]{2,1,0:T(8,128)}, u32[]{:S(2)}) copy-start(f32[16,64,64]{2,1,0:T(8,128)} %reshape.81) | copy-start | bytes 786436
  41.2 5.1 %copy-start.10 = (s32[1,2]{1,0:T(1,128)S(1)}, s32[1,2]{1,0:T(1,128)}, u32[]{:S(2)}) copy-start(s32[1,2]{1,0:T(1,128)} %param.15) | copy-start | bytes 28
  42.6 18.8 %copy-start.1 = (f32[1,2,6,4096]{3,1,2,0:T(2,128)S(1)}, f32[1,2,6,4096]{3,1,2,0:T(2,128)}, u32[]{:S(2)}) copy-start(f32[1,2,6,4096]{3,1,2,0:T(2,128)} %param.10) | copy-start | bytes 589828
  42.6 18.4 %all-to-all-start.1 = ((f32[16,2,4096]{2,1,0:T(2,128)}), f32[16,2,4096]{2,1,0:T(2,128)S(1)}, u32[]{:S(2)}, u32[]{:S(2)}) async-start(f32[16,2,4096]{2,1,0:T(2,128)} %dynamic_update_slice.4.clone), calls=%async_computation.1 | async-start | bytes 1048576 | tf_op jit(solution)/shard_map/all_to_all | solution.py:73
